TPU v7x, 32 devices: a 4x4x1 block of a 4x4x8 slice. The times are simulated.
32 devices in a mesh: dp: 2 (over z, core), tp: 16 (over x, y).
Axes of the slice: x: 4, y: 4, z: 1, core: 2. Of those that a mesh axis runs over, the one named last changes fastest.
The devices are a block of a 4x4x8 slice.
Arguments:
- x: bfloat16 [5120, 7168], P(('dp', 'tp')), parts along dimension 0
- w_gate: bfloat16 [7168, 20480], P(None, 'tp')
- w_up: bfloat16 [7168, 20480], P(None, 'tp')
- w_down: bfloat16 [20480, 7168], P('tp')
Outputs:
- output: bfloat16 [5120, 7168], P(('dp', 'tp')), parts along dimension 0
There are 2 independent parts. A program takes and returns all parts, laid end to end along the dimension named above; an argument that names none is the same for every part.
All inputs are finite; a program needn't handle non-finite values.
Results may differ from a plain program's by a relative error of at most 0.016.
Values are sent between devices in bfloat16 or wider.
A program may use at most 768 MiB of HBM per device.

v0:
```python
import jax
import jax.numpy as jnp
from jax import lax
from jax.sharding import PartitionSpec as P


def solution(mesh):
    def step(x, w_gate, w_up, w_down):
        rows = lax.all_gather(x, "tp", axis=0, tiled=True)
        gate = jnp.dot(rows, w_gate, preferred_element_type=jnp.float32)
        up = jnp.dot(rows, w_up, preferred_element_type=jnp.float32)
        hidden = (jax.nn.silu(gate) * up).astype(jnp.bfloat16)
        term = jnp.dot(hidden, w_down, preferred_element_type=jnp.float32).astype(jnp.bfloat16)
        return lax.psum_scatter(term, "tp", scatter_dimension=0, tiled=True)

    return jax.shard_map(
        step,
        mesh=mesh,
        in_specs=(P(("dp", "tp"), None), P(None, "tp"), P(None, "tp"), P("tp", None)),
        out_specs=P(("dp", "tp"), None),
        check_vma=False,
    )
```

profile of v0, /device:TPU:97, one launch (start us, length us, event | category | flops | bytes accessed | tf_op | source)
XLA Modules:
  0.0 604.9 jit_solution(3108098712845408985)
XLA Ops:
  6.5 0.0 all-gather.2.cloned.1.call-start
  6.6 0.7 all-gather.2.cloned.1.call-update
  7.3 0.1 reduce-scatter.2.cloned.1.call-start
  7.4 213.6 %all-gather.2.cloned.1.call-done = bf16[2560,7168]{1,0:T(8,128)(2,1)} async-done(((bf16[160,7168]{1,0:T(8,128)(2,1)}), bf16[2560,7168]{1,0:T(8,128)(2,1)}) %all-gather.2.cloned.1.call-update) | async-done | bytes 36700176 | tf_op jit(solution)/shard_map/all_gather | solution.py:9
  220.9 57.9 %fusion.1 = f32[2560,1280]{1,0:T(8,128)} fusion(bf16[2560,7168]{1,0:T(8,128)(2,1)} %all-gather.2.cloned.1.call-done, bf16[7168,1280]{1,0:T(8,128)(2,1)} %param.5), kind=kOutput, calls=%fused_computation.3 | convolution fusion | flops 46976204800 | bytes 68157440 | tf_op jit(solution)/shard_map/dot_general | solution.py:10
  278.8 57.7 %fusion = bf16[2560,1280]{1,0:T(8,128)(2,1)S(1)} fusion(bf16[2560,7168]{1,0:T(8,128)(2,1)} %all-gather.2.cloned.1.call-done, bf16[7168,1280]{1,0:T(8,128)(2,1)} %param.6, f32[2560,1280]{1,0:T(8,128)} %fusion.1), kind=kOutput, calls=%fused_computation.2 | convolution fusion | flops 46995865600 | bytes 74711040 | tf_op jit(solution)/shard_map/dot_general | solution.py:11
  336.5 56.5 %convolution_convert_fusion = bf16[2560,7168]{1,0:T(8,128)(2,1)} fusion(bf16[2560,1280]{1,0:T(8,128)(2,1)S(1)} %fusion, bf16[1280,7168]{1,0:T(8,128)(2,1)} %param.7), kind=kOutput, calls=%fused_computation | convolution fusion | flops 46994554880 | bytes 61603840 | tf_op jit(solution)/shard_map/dot_general | solution.py:13
  393.0 0.1 reduce-scatter.2.cloned.1.call-update
  393.0 205.0 %reduce-scatter.2.cloned.1.call-done = bf16[160,7168]{1,0:T(8,128)(2,1)} async-done(((bf16[2560,7168]{1,0:T(8,128)(2,1)}), bf16[160,7168]{1,0:T(8,128)(2,1)}) %reduce-scatter.2.cloned.1.call-update) | async-done | bytes 2293776 | tf_op jit(solution)/shard_map/reduce_scatter | solution.py:14
Async XLA Ops:
  6.5 214.4 %all-gather.2.cloned.1.call-start = ((), (), s32[]{:S(2)}) async-start(), calls=%async_computation.1 | async-start | bytes 38993920 | tf_op jit(solution)/shard_map/all_gather | solution.py:9
  7.3 590.7 %reduce-scatter.2.cloned.1.call-start = ((), (), s32[]{:S(2)}) async-start(), calls=%async_computation.2 | async-start | bytes 38993920 | tf_op jit(solution)/shard_map/reduce_scatter | solution.py:14
Sparse Core Ops, SparseCore 0:
  9.3 211.5 all-gather.1
  393.1 204.8 reduce-scatter.1
where the time goes:
time: 605 us
  waiting for transfers between devices  419 us (69%)
  matrix products  172 us (28%)
  between operations  13.4 us (2%)
    all_gather x1, waiting for transfers between devices, step(): rows = lax.all_gather(x, 'tp', axis=0, tiled=True)  214 us
    reduce_scatter x1, waiting for transfers between devices, step(): return lax.psum_scatter(term, 'tp', scatter_dimension=0, tiled=True)  205 us
    dot_general x1, matrix products, step(): gate = jnp.dot(rows, w_gate, preferred_element_type=jnp.float32)  57.9 us
    dot_general x1, matrix products, step(): up = jnp.dot(rows, w_up, preferred_element_type=jnp.float32)  57.7 us
    dot_general x1, matrix products, step(): jnp.dot(hidden, w_down, preferred_element_type=jnp.float32)  56.5 us
  transfers between devices with their start and end apart: 2, of which 2 were waited for; matrix products, arithmetic and copies ran while one was open for 0% of the time, Pallas kernels for 0%

commit v1 on v0

v1 whole, which is shorter than its diff:
```python
import functools
import math

import jax
import jax.numpy as jnp
from jax import lax
from jax.experimental import pallas as pl
from jax.experimental.pallas import tpu as pltpu
from jax.sharding import PartitionSpec as P

OFF = (0, 1, -1, 2)
PLUS, MINUS = 1, 2
UNITS = 8
VMEM_LIMIT = 67043328


def place(h, k, j):
    if k == 0:
        return h, j
    if k < 3:
        return 2 + j, 2 * h + k - 1
    return 6 + j // 2, 2 * h + j % 2


class Sems:
    def __init__(self):
        self.ids = {}

    def __call__(self, key):
        return self.ids.setdefault(key, len(self.ids))


def message_ids():
    ids = Sems()
    for h in (0, 1):
        for d in (0, 1):
            ids(("a", h, d)), ids(("af", h, d))
            for j in range(4):
                ids(("b", h, j, d)), ids(("bf", h, j, d))
            for k in range(4):
                for m in (1, 2, 3):
                    ids(("ra", h, k, d, m))
            for m in (1, 2, 3):
                ids(("rb", h, d, m))
    return ids.ids


IDS = message_ids()


def kernel(
    side, x, wg_hbm, wu_hbm, wd_hbm,
    y, xg, tf, tb, a1, bx, m3, rf, rb, a1b, bxb, m3b,
    wg, wu, wd, xbuf, hid, stg, fa, wsem, xsem, osem, ssem, lsem, send, recv,
):
    half, depth = x.shape[0] // 2, x.shape[1]
    piece = depth // 2
    ff = wg_hbm.shape[1]
    me = lax.axis_index("tp")
    mx, my = me // side, me % side

    def peer(h, second, d):
        step = 1 if d == 0 else side - 1
        if (h == 0) != second:
            return ((mx + step) % side) * side + my
        return mx * side + (my + step) % side

    def col(c):
        return pl.ds(c * piece, piece)

    def rows(s):
        return pl.ds(s * half, half)

    def blk(buf, h, k, j, c=None):
        u, s = place(h, k, j)
        if c is None:
            return buf.at[u, rows(s), :]
        return buf.at[u, rows(s), col(c)]

    def message(key):
        kind, h, d = key[0], key[1], key[3] if key[0] in ("b", "bf", "ra") else key[2]
        second = kind in ("b", "bf", "rb")
        here = PLUS if d == 0 else MINUS
        back = MINUS if d == 0 else PLUS
        if kind == "a":
            src, dst = x.at[rows(h), :], blk(xg, h, 0, back)
        elif kind == "af":
            src, dst = blk(xg, h, 0, back, d), blk(xg, h, 0, 3, d)
        elif kind == "b":
            j = key[2]
            src = x.at[rows(h), :] if j == 0 else blk(xg, h, 0, j)
            dst = blk(xg, h, back, j)
        elif kind == "bf":
            j = key[2]
            src, dst = blk(xg, h, back, j, d), blk(xg, h, 3, j, d)
        elif kind == "ra":
            k, m = key[2], key[4]
            if m == 1:
                src, dst = blk(tb, h, k, 3, d), a1.at[h, k, d]
            elif m == 2:
                src, dst = blk(tb, h, k, here, 1 - d), bx.at[h, k, d, :, col(1 - d)]
            else:
                src, dst = m3.at[h, k, d], bx.at[h, k, d, :, col(d)]
        else:
            m = key[3]
            if m == 1:
                src, dst = rb.at[h, 3, :, col(d)], a1b.at[h, d]
            elif m == 2:
                src, dst = rb.at[h, here, :, col(1 - d)], bxb.at[h, d, :, col(1 - d)]
            else:
                src, dst = m3b.at[h, d], bxb.at[h, d, :, col(d)]
        i = IDS[key]
        return pltpu.make_async_remote_copy(
            src_ref=src,
            dst_ref=dst,
            send_sem=send.at[i],
            recv_sem=recv.at[i],
            device_id={"tp": peer(h, second, d)},
            device_id_type=pl.DeviceIdType.MESH,
        )

    both = [(h, d) for h in (0, 1) for d in (0, 1)]

    barrier = pltpu.get_barrier_semaphore()
    for h, d in both:
        pl.semaphore_signal(
            barrier, inc=1, device_id={"tp": peer(h, False, d)},
            device_id_type=pl.DeviceIdType.MESH,
        )
    pl.semaphore_wait(barrier, 4)

    for h, d in both:
        message(("a", h, d)).start()
    weights = [
        pltpu.make_async_copy(src, dst, wsem.at[i])
        for i, (src, dst) in enumerate(((wg_hbm, wg), (wu_hbm, wu), (wd_hbm, wd)))
    ]
    own = [
        pltpu.make_async_copy(x.at[rows(h), :], xbuf.at[rows(h), :], lsem.at[h]) for h in (0, 1)
    ]
    keep = [
        pltpu.make_async_copy(xbuf.at[rows(h), :], blk(xg, h, 0, 0), lsem.at[h]) for h in (0, 1)
    ]
    for c in own:
        c.start()
    for c in own:
        c.wait()
    for c in keep:
        c.start()
    for c in weights:
        c.start()
    for c in keep:
        c.wait()
    for h, d in both:
        message(("a", h, d)).wait_recv()
        message(("af", h, d)).start()
    for j in range(3):
        for h, d in both:
            message(("b", h, j, d)).start()
    for c in weights:
        c.wait()
    for h, d in both:
        message(("af", h, d)).wait_recv()
    for h, d in both:
        message(("b", h, 3, d)).start()

    def send_terms(k):
        for m in (1, 2):
            for h, d in both:
                message(("ra", h, k, d, m)).start()

    def before(u):
        for j in range(4):
            @pl.when(u == 2 + j)
            def _():
                for h, d in both:
                    message(("b", h, j, d)).wait_recv()
                for h, d in both:
                    message(("bf", h, j, d)).start()
                if j == 3:
                    send_terms(0)

        for part in (0, 1):
            @pl.when(u == 6 + part)
            def _():
                if part == 0:
                    send_terms(PLUS)
                    send_terms(MINUS)
                for j in (2 * part, 2 * part + 1):
                    for h, d in both:
                        message(("bf", h, j, d)).wait_recv()

    n_up, n_down = 256, stg.shape[2]

    def stage(u, t, slot):
        c = pl.ds(pl.multiple_of(t * n_down, n_down), n_down)
        return pltpu.make_async_copy(stg.at[slot], tf.at[u, :, c], osem.at[slot])

    def unit(u, carry):
        before(u)
        load = pltpu.make_async_copy(xg.at[u], xbuf, xsem)
        load.start()
        load.wait()

        def up_tile(t, carry):
            c = pl.ds(pl.multiple_of(t * n_up, n_up), n_up)
            gate = jnp.dot(xbuf[...], wg[:, c], preferred_element_type=jnp.float32)
            up = jnp.dot(xbuf[...], wu[:, c], preferred_element_type=jnp.float32)
            hid[:, c] = (jax.nn.silu(gate) * up).astype(jnp.bfloat16)
            return carry

        lax.fori_loop(0, ff // n_up, up_tile, 0)
        n = depth // n_down

        def down_tile(t, carry):
            slot = t % 2

            @pl.when(t >= 2)
            def _():
                stage(u, t - 2, slot).wait()

            c = pl.ds(pl.multiple_of(t * n_down, n_down), n_down)
            term = jnp.dot(hid[...], wd[:, c], preferred_element_type=jnp.float32)
            stg[slot] = term
            xbuf[:, c] = term.astype(jnp.bfloat16)
            stage(u, t, slot).start()
            return carry

        lax.fori_loop(0, n, down_tile, 0)
        out = pltpu.make_async_copy(xbuf, tb.at[u], ssem)
        out.start()
        for t in (n - 2, n - 1):
            stage(u, t, t % 2).wait()
        out.wait()
        return carry

    lax.fori_loop(0, UNITS, unit, 0)

    def room(i):
        return xbuf.at[rows(i // 2), col(i % 2)]

    def combine(items):
        def loads(i):
            wide, narrow, _, _ = items[i]
            s = i % 2
            out = [pltpu.make_async_copy(wide, fa.at[s], lsem.at[3 * s])]
            for n, ref in enumerate(narrow):
                out.append(pltpu.make_async_copy(ref, room(3 * s + n), lsem.at[3 * s + 1 + n]))
            return out

        def stores(i):
            _, _, wide, narrow = items[i]
            s = i % 2
            out = []
            if wide is not None:
                out.append(pltpu.make_async_copy(fa.at[s], wide, osem.at[s]))
            if narrow is not None:
                out.append(pltpu.make_async_copy(room(3 * s + 2), narrow, osem.at[2 + s]))
            return out

        for c in loads(0):
            c.start()
        for i in range(len(items)):
            s = i % 2
            if i + 1 < len(items):
                if i >= 1:
                    for c in stores(i - 1):
                        c.wait()
                for c in loads(i + 1):
                    c.start()
            for c in loads(i):
                c.wait()
            total = fa[s]
            for n in range(len(items[i][1])):
                r = 3 * s + n
                total = total + xbuf[rows(r // 2), col(r % 2)].astype(jnp.float32)
            if items[i][2] is not None:
                fa[s] = total
            if items[i][3] is not None:
                r = 3 * s + 2
                xbuf[rows(r // 2), col(r % 2)] = total.astype(jnp.bfloat16)
            for c in stores(i):
                c.start()
        for i in range(max(0, len(items) - 2), len(items)):
            for c in stores(i):
                c.wait()

    def pass_on(k):
        for h, d in both:
            message(("ra", h, k, d, 1)).wait_recv()
        combine([
            (blk(tf, h, k, PLUS if d == 0 else MINUS, d), [a1.at[h, k, d]], None, m3.at[h, k, d])
            for h, d in both
        ])
        for h, d in both:
            message(("ra", h, k, d, 3)).start()

    def first_sum(k, wide, narrow):
        for h, d in both:
            for m in (2, 3):
                message(("ra", h, k, d, m)).wait_recv()
        combine([
            (
                blk(tf, h, k, 0, c),
                [bx.at[h, k, 0, :, col(c)], bx.at[h, k, 1, :, col(c)]],
                rf.at[h, k, :, col(c)] if c in wide else None,
                rb.at[h, k, :, col(c)] if c in narrow else None,
            )
            for h in (0, 1) for c in (0, 1)
        ])

    send_terms(3)
    pass_on(0)
    pass_on(PLUS)
    pass_on(3)
    pass_on(MINUS)
    first_sum(0, (0, 1), ())
    first_sum(PLUS, (0,), (1,))
    for h in (0, 1):
        message(("rb", h, 0, 2)).start()
    first_sum(3, (), (0, 1))
    for h, d in both:
        message(("rb", h, d, 1)).start()
    first_sum(MINUS, (1,), (0,))
    for h in (0, 1):
        message(("rb", h, 1, 2)).start()
    for h, d in both:
        message(("rb", h, d, 1)).wait_recv()
    combine([
        (rf.at[h, PLUS if d == 0 else MINUS, :, col(d)], [a1b.at[h, d]], None, m3b.at[h, d])
        for h, d in both
    ])
    for h, d in both:
        message(("rb", h, d, 3)).start()
    for h, d in both:
        for m in (2, 3):
            message(("rb", h, d, m)).wait_recv()
    combine([
        (
            rf.at[h, 0, :, col(c)],
            [bxb.at[h, 0, :, col(c)], bxb.at[h, 1, :, col(c)]],
            None,
            y.at[rows(h), col(c)],
        )
        for h in (0, 1) for c in (0, 1)
    ])
    for key in IDS:
        message(key).wait_send()


def solution(mesh):
    side = math.isqrt(mesh.shape["tp"])

    def step(x, w_gate, w_up, w_down):
        rows, depth = x.shape
        ff = w_gate.shape[1]
        half, piece = rows // 2, depth // 2
        bf, f32 = jnp.bfloat16, jnp.float32
        n = len(IDS)
        flops = 6 * rows * side * side * depth * ff
        shapes = [
            ((rows, depth), bf),
            ((UNITS, 4 * half, depth), bf),
            ((UNITS, 4 * half, depth), f32),
            ((UNITS, 4 * half, depth), bf),
            ((2, 4, 2, half, piece), bf),
            ((2, 4, 2, half, depth), bf),
            ((2, 4, 2, half, piece), bf),
            ((2, 4, half, depth), f32),
            ((2, 4, half, depth), bf),
            ((2, 2, half, piece), bf),
            ((2, 2, half, depth), bf),
            ((2, 2, half, piece), bf),
        ]
        out = pl.pallas_call(
            functools.partial(kernel, side),
            out_shape=[jax.ShapeDtypeStruct(s, t) for s, t in shapes],
            in_specs=[pl.BlockSpec(memory_space=pl.ANY)] * 4,
            out_specs=[pl.BlockSpec(memory_space=pl.ANY)] * len(shapes),
            scratch_shapes=[
                pltpu.VMEM((depth, ff), bf),
                pltpu.VMEM((depth, ff), bf),
                pltpu.VMEM((ff, depth), bf),
                pltpu.VMEM((4 * half, depth), bf),
                pltpu.VMEM((4 * half, ff), bf),
                pltpu.VMEM((2, 4 * half, depth // 7), f32),
                pltpu.VMEM((2, half, piece), f32),
                pltpu.SemaphoreType.DMA((3,)),
                pltpu.SemaphoreType.DMA,
                pltpu.SemaphoreType.DMA((4,)),
                pltpu.SemaphoreType.DMA,
                pltpu.SemaphoreType.DMA((6,)),
                pltpu.SemaphoreType.DMA((n,)),
                pltpu.SemaphoreType.DMA((n,)),
            ],
            compiler_params=pltpu.CompilerParams(
                collective_id=0, has_side_effects=True, vmem_limit_bytes=VMEM_LIMIT
            ),
            cost_estimate=pl.CostEstimate(
                flops=flops, bytes_accessed=3 * depth * ff * 2, transcendentals=0
            ),
            name="block",
        )(x, w_gate, w_up, w_down)
        return out[0]

    return jax.shard_map(
        step,
        mesh=mesh,
        in_specs=(P(("dp", "tp"), None), P(None, "tp"), P(None, "tp"), P("tp", None)),
        out_specs=P(("dp", "tp"), None),
        check_vma=False,
    )
```

time: 605 us -> 397 us (0.66)
  waiting for transfers between devices: 419 us -> 0 us
  Pallas kernels: 0 us -> 393 us
  matrix products: 172 us -> 0 us
  between operations: 13.4 us -> 0.01 us
    pallas_call x0 -> x1, Pallas kernels: none -> 393 us  [step(): pl.pallas_call(functools.partial(kernel, side), out_shape=[jax.ShapeDtype...]
    all_gather x1 -> x0, waiting for transfers between devices: 214 us -> none  [step(): rows = lax.all_gather(x, 'tp', axis=0, tiled=True)]
    reduce_scatter x1 -> x0, waiting for transfers between devices: 205 us -> none  [step(): return lax.psum_scatter(term, 'tp', scatter_dimension=0, tiled=True)]
    dot_general x3 -> x0, matrix products: 172 us -> none  [the longest x1 57.9 us: step(): gate = jnp.dot(rows, w_gate, preferred_element_type=jnp.float32)]
  transfers between devices with their start and end apart: 2 -> 0, of which waited for: 2 -> 0; matrix products, arithmetic and copies ran while one was open for 0% -> 0% of each run, Pallas kernels for 0% -> 0%
where the time goes in v1:
time: 397 us; the launch traced here: 396 us
  Pallas kernels  393 us (99%)
    pallas_call x1, Pallas kernels, step(): pl.pallas_call(functools.partial(kernel, side), out_shape=[jax.ShapeDtype...  393 us

profile of v1, /device:TPU:97, one launch (start us, length us, event | category | flops | bytes accessed | tf_op | source)
XLA Modules:
  0.0 396.1 jit_solution(11096235081270931222)
XLA Ops:
  0.0 392.9 %block.1 = (bf16[160,7168]{1,0:T(8,128)(2,1)}, bf16[8,320,7168]{2,1,0:T(8,128)(2,1)}, f32[8,320,7168]{2,1,0:T(8,128)}, bf16[8,320,7168]{2,1,0:T(8,128)(2,1)}, bf...) custom-call(bf16[160,7168]{1,0:T(8,128)(2,1)} %x.1, ...), custom_call_target="tpu_custom_call" | custom-call | flops 140928614400 | bytes 55050240 | tf_op jit(solution)/shard_map/block/pallas_call | solution.py:375
  392.9 3.2 copy.6

commit v2 on v1

--- a/solution.py
+++ b/solution.py
@@ -34,7 +34,9 @@
     ids = Sems()
     for h in (0, 1):
         for d in (0, 1):
-            ids(("a", h, d)), ids(("af", h, d))
+            ids(("af", h, d))
+            for c in (0, 1):
+                ids(("a", h, d, c))
             for j in range(4):
                 ids(("b", h, j, d)), ids(("bf", h, j, d))
             for k in range(4):
@@ -50,12 +52,13 @@
 
 def kernel(
     side, x, wg_hbm, wu_hbm, wd_hbm,
-    y, xg, tf, tb, a1, bx, m3, rf, rb, a1b, bxb, m3b,
-    wg, wu, wd, xbuf, hid, stg, fa, wsem, xsem, osem, ssem, lsem, send, recv,
+    own_sum, low, high, xg, tf, tb, a1, bx, m3, rf, rb, a1b, m3b,
+    wg, wu, wd, xbuf, hid, stg, half_stg, fa, wsem, xsem, osem, ssem, lsem, send, recv,
 ):
     half, depth = x.shape[0] // 2, x.shape[1]
     piece = depth // 2
     ff = wg_hbm.shape[1]
+    sides = (low, high)
     me = lax.axis_index("tp")
     mx, my = me // side, me % side
 
@@ -83,7 +86,8 @@
         here = PLUS if d == 0 else MINUS
         back = MINUS if d == 0 else PLUS
         if kind == "a":
-            src, dst = x.at[rows(h), :], blk(xg, h, 0, back)
+            c = key[3]
+            src, dst = x.at[rows(h), col(c)], blk(xg, h, 0, back, c)
         elif kind == "af":
             src, dst = blk(xg, h, 0, back, d), blk(xg, h, 0, 3, d)
         elif kind == "b":
@@ -106,9 +110,9 @@
             if m == 1:
                 src, dst = rb.at[h, 3, :, col(d)], a1b.at[h, d]
             elif m == 2:
-                src, dst = rb.at[h, here, :, col(1 - d)], bxb.at[h, d, :, col(1 - d)]
+                src, dst = rb.at[h, here, :, col(1 - d)], sides[d].at[rows(h), col(1 - d)]
             else:
-                src, dst = m3b.at[h, d], bxb.at[h, d, :, col(d)]
+                src, dst = m3b.at[h, d], sides[d].at[rows(h), col(d)]
         i = IDS[key]
         return pltpu.make_async_remote_copy(
             src_ref=src,
@@ -129,8 +133,9 @@
         )
     pl.semaphore_wait(barrier, 4)
 
-    for h, d in both:
-        message(("a", h, d)).start()
+    for n in (0, 1):
+        for h, d in both:
+            message(("a", h, d, (d + n) % 2)).start()
     weights = [
         pltpu.make_async_copy(src, dst, wsem.at[i])
         for i, (src, dst) in enumerate(((wg_hbm, wg), (wu_hbm, wu), (wd_hbm, wd)))
@@ -152,9 +157,13 @@
     for c in keep:
         c.wait()
     for h, d in both:
-        message(("a", h, d)).wait_recv()
+        message(("a", h, d, d)).wait_recv()
         message(("af", h, d)).start()
-    for j in range(3):
+    for h, d in both:
+        message(("b", h, 0, d)).start()
+    for h, d in both:
+        message(("a", h, d, 1 - d)).wait_recv()
+    for j in (PLUS, MINUS):
         for h, d in both:
             message(("b", h, j, d)).start()
     for c in weights:
@@ -169,21 +178,20 @@
             for h, d in both:
                 message(("ra", h, k, d, m)).start()
 
-    def before(u):
+    def arrivals(u):
         for j in range(4):
-            @pl.when(u == 2 + j)
+            @pl.when(u == 1 + j)
             def _():
                 for h, d in both:
                     message(("b", h, j, d)).wait_recv()
-                for h, d in both:
                     message(("bf", h, j, d)).start()
                 if j == 3:
                     send_terms(0)
 
         for part in (0, 1):
-            @pl.when(u == 6 + part)
+            @pl.when(u == 5 + part)
             def _():
-                if part == 0:
+                if part == 1:
                     send_terms(PLUS)
                     send_terms(MINUS)
                 for j in (2 * part, 2 * part + 1):
@@ -191,16 +199,27 @@
                         message(("bf", h, j, d)).wait_recv()
 
     n_up, n_down = 256, stg.shape[2]
+    n = depth // n_down
 
     def stage(u, t, slot):
         c = pl.ds(pl.multiple_of(t * n_down, n_down), n_down)
-        return pltpu.make_async_copy(stg.at[slot], tf.at[u, :, c], osem.at[slot])
+        return (
+            pltpu.make_async_copy(stg.at[slot], tf.at[u, :, c], osem.at[slot]),
+            pltpu.make_async_copy(half_stg.at[slot], tb.at[u, :, c], ssem.at[slot]),
+        )
+
+    def drain(u):
+        for t in (n - 2, n - 1):
+            for c in stage(u, t, t % 2):
+                c.wait()
+
+    def load(u):
+        return pltpu.make_async_copy(xg.at[u], xbuf, xsem)
+
+    load(0).start()
 
     def unit(u, carry):
-        before(u)
-        load = pltpu.make_async_copy(xg.at[u], xbuf, xsem)
-        load.start()
-        load.wait()
+        load(u).wait()
 
         def up_tile(t, carry):
             c = pl.ds(pl.multiple_of(t * n_up, n_up), n_up)
@@ -210,92 +229,114 @@
             return carry
 
         lax.fori_loop(0, ff // n_up, up_tile, 0)
-        n = depth // n_down
+
+        @pl.when(u > 0)
+        def _():
+            drain(u - 1)
+
+        arrivals(u)
+
+        @pl.when(u < UNITS - 1)
+        def _():
+            load(u + 1).start()
 
         def down_tile(t, carry):
             slot = t % 2
 
             @pl.when(t >= 2)
             def _():
-                stage(u, t - 2, slot).wait()
+                for c in stage(u, t - 2, slot):
+                    c.wait()
 
             c = pl.ds(pl.multiple_of(t * n_down, n_down), n_down)
             term = jnp.dot(hid[...], wd[:, c], preferred_element_type=jnp.float32)
             stg[slot] = term
-            xbuf[:, c] = term.astype(jnp.bfloat16)
-            stage(u, t, slot).start()
+            half_stg[slot] = term.astype(jnp.bfloat16)
+            for c in stage(u, t, slot):
+                c.start()
             return carry
 
         lax.fori_loop(0, n, down_tile, 0)
-        out = pltpu.make_async_copy(xbuf, tb.at[u], ssem)
-        out.start()
-        for t in (n - 2, n - 1):
-            stage(u, t, t % 2).wait()
-        out.wait()
         return carry
 
     lax.fori_loop(0, UNITS, unit, 0)
+    drain(UNITS - 1)
+
+    quarter = fa.shape[2]
 
     def room(i):
-        return xbuf.at[rows(i // 2), col(i % 2)]
+        return rows(i // 4), pl.ds((i % 4) * quarter, quarter)
 
     def combine(items):
+        parts = []
+        for wide, narrow, to_wide, to_narrow, then in items:
+            for q in (0, 1):
+                c = pl.ds(q * quarter, quarter)
+                cut = lambda ref: None if ref is None else ref.at[:, c]
+                parts.append((
+                    cut(wide), [cut(r) for r in narrow], cut(to_wide), cut(to_narrow),
+                    then if q == 1 else None,
+                ))
+
         def loads(i):
-            wide, narrow, _, _ = items[i]
+            wide, narrow = parts[i][:2]
             s = i % 2
             out = [pltpu.make_async_copy(wide, fa.at[s], lsem.at[3 * s])]
             for n, ref in enumerate(narrow):
-                out.append(pltpu.make_async_copy(ref, room(3 * s + n), lsem.at[3 * s + 1 + n]))
+                out.append(pltpu.make_async_copy(
+                    ref, xbuf.at[room(3 * s + n)], lsem.at[3 * s + 1 + n]))
             return out
 
         def stores(i):
-            _, _, wide, narrow = items[i]
+            wide, narrow = parts[i][2:4]
             s = i % 2
             out = []
             if wide is not None:
                 out.append(pltpu.make_async_copy(fa.at[s], wide, osem.at[s]))
             if narrow is not None:
-                out.append(pltpu.make_async_copy(room(3 * s + 2), narrow, osem.at[2 + s]))
+                out.append(pltpu.make_async_copy(xbuf.at[room(3 * s + 2)], narrow, ssem.at[s]))
             return out
+
+        def finish(i):
+            for c in stores(i):
+                c.wait()
+            if parts[i][4] is not None:
+                parts[i][4].start()
 
         for c in loads(0):
             c.start()
-        for i in range(len(items)):
+        for i in range(len(parts)):
             s = i % 2
-            if i + 1 < len(items):
-                if i >= 1:
-                    for c in stores(i - 1):
-                        c.wait()
+            if i >= 1:
+                finish(i - 1)
+            if i + 1 < len(parts):
                 for c in loads(i + 1):
                     c.start()
             for c in loads(i):
                 c.wait()
             total = fa[s]
-            for n in range(len(items[i][1])):
-                r = 3 * s + n
-                total = total + xbuf[rows(r // 2), col(r % 2)].astype(jnp.float32)
-            if items[i][2] is not None:
+            for n in range(len(parts[i][1])):
+                total = total + xbuf[room(3 * s + n)].astype(jnp.float32)
+            if parts[i][2] is not None:
                 fa[s] = total
-            if items[i][3] is not None:
-                r = 3 * s + 2
-                xbuf[rows(r // 2), col(r % 2)] = total.astype(jnp.bfloat16)
+            if parts[i][3] is not None:
+                xbuf[room(3 * s + 2)] = total.astype(jnp.bfloat16)
             for c in stores(i):
                 c.start()
-        for i in range(max(0, len(items) - 2), len(items)):
-            for c in stores(i):
-                c.wait()
+        finish(len(parts) - 1)
 
     def pass_on(k):
         for h, d in both:
             message(("ra", h, k, d, 1)).wait_recv()
         combine([
-            (blk(tf, h, k, PLUS if d == 0 else MINUS, d), [a1.at[h, k, d]], None, m3.at[h, k, d])
+            (
+                blk(tf, h, k, PLUS if d == 0 else MINUS, d), [a1.at[h, k, d]],
+                None, m3.at[h, k, d], message(("ra", h, k, d, 3)),
+            )
             for h, d in both
         ])
-        for h, d in both:
-            message(("ra", h, k, d, 3)).start()
-
-    def first_sum(k, wide, narrow):
+
+    def first_sum(k, wide, narrow, then=lambda h, c: None):
         for h, d in both:
             for m in (2, 3):
                 message(("ra", h, k, d, m)).wait_recv()
@@ -303,8 +344,10 @@
             (
                 blk(tf, h, k, 0, c),
                 [bx.at[h, k, 0, :, col(c)], bx.at[h, k, 1, :, col(c)]],
-                rf.at[h, k, :, col(c)] if c in wide else None,
+                (own_sum.at[rows(h), col(c)] if k == 0 else rf.at[h, k, :, col(c)])
+                if c in wide else None,
                 rb.at[h, k, :, col(c)] if c in narrow else None,
+                then(h, c),
             )
             for h in (0, 1) for c in (0, 1)
         ])
@@ -316,34 +359,22 @@
     pass_on(MINUS)
     first_sum(0, (0, 1), ())
     first_sum(PLUS, (0,), (1,))
+    first_sum(3, (), (0, 1), lambda h, c: message(("rb", h, c, 1)))
     for h in (0, 1):
         message(("rb", h, 0, 2)).start()
-    first_sum(3, (), (0, 1))
-    for h, d in both:
-        message(("rb", h, d, 1)).start()
-    first_sum(MINUS, (1,), (0,))
-    for h in (0, 1):
-        message(("rb", h, 1, 2)).start()
+    first_sum(MINUS, (1,), (0,), lambda h, c: message(("rb", h, 1, 2)) if c == 0 else None)
     for h, d in both:
         message(("rb", h, d, 1)).wait_recv()
     combine([
-        (rf.at[h, PLUS if d == 0 else MINUS, :, col(d)], [a1b.at[h, d]], None, m3b.at[h, d])
+        (
+            rf.at[h, PLUS if d == 0 else MINUS, :, col(d)], [a1b.at[h, d]],
+            None, m3b.at[h, d], message(("rb", h, d, 3)),
+        )
         for h, d in both
     ])
     for h, d in both:
-        message(("rb", h, d, 3)).start()
-    for h, d in both:
         for m in (2, 3):
             message(("rb", h, d, m)).wait_recv()
-    combine([
-        (
-            rf.at[h, 0, :, col(c)],
-            [bxb.at[h, 0, :, col(c)], bxb.at[h, 1, :, col(c)]],
-            None,
-            y.at[rows(h), col(c)],
-        )
-        for h in (0, 1) for c in (0, 1)
-    ])
     for key in IDS:
         message(key).wait_send()
 
@@ -359,6 +390,8 @@
         n = len(IDS)
         flops = 6 * rows * side * side * depth * ff
         shapes = [
+            ((rows, depth), f32),
+            ((rows, depth), bf),
             ((rows, depth), bf),
             ((UNITS, 4 * half, depth), bf),
             ((UNITS, 4 * half, depth), f32),
@@ -369,7 +402,6 @@
             ((2, 4, half, depth), f32),
             ((2, 4, half, depth), bf),
             ((2, 2, half, piece), bf),
-            ((2, 2, half, depth), bf),
             ((2, 2, half, piece), bf),
         ]
         out = pl.pallas_call(
@@ -384,11 +416,12 @@
                 pltpu.VMEM((4 * half, depth), bf),
                 pltpu.VMEM((4 * half, ff), bf),
                 pltpu.VMEM((2, 4 * half, depth // 7), f32),
-                pltpu.VMEM((2, half, piece), f32),
+                pltpu.VMEM((2, 4 * half, depth // 7), bf),
+                pltpu.VMEM((2, half, piece // 2), f32),
                 pltpu.SemaphoreType.DMA((3,)),
                 pltpu.SemaphoreType.DMA,
-                pltpu.SemaphoreType.DMA((4,)),
-                pltpu.SemaphoreType.DMA,
+                pltpu.SemaphoreType.DMA((2,)),
+                pltpu.SemaphoreType.DMA((2,)),
                 pltpu.SemaphoreType.DMA((6,)),
                 pltpu.SemaphoreType.DMA((n,)),
                 pltpu.SemaphoreType.DMA((n,)),
@@ -401,7 +434,8 @@
             ),
             name="block",
         )(x, w_gate, w_up, w_down)
-        return out[0]
+        own_sum, low, high = out[:3]
+        return (own_sum + low.astype(f32) + high.astype(f32)).astype(bf)
 
     return jax.shard_map(
         step,

time: 397 us -> 386 us (0.972)
  Pallas kernels: 393 us -> 379 us
  other arithmetic: 0 us -> 5.96 us
    pallas_call x1, Pallas kernels: 393 us -> 379 us  [step(): pl.pallas_call(functools.partial(kernel, side), out_shape=[jax.ShapeDtype...]
    convert_element_type x0 -> x1, other arithmetic: none -> 5.96 us  [step(): return (own_sum + low.astype(f32) + high.astype(f32)).astype(bf)]
where the time goes in v2:
time: 386 us; the launch traced here: 385 us
  Pallas kernels  379 us (98%)
  other arithmetic  5.96 us (2%)
    pallas_call x1, Pallas kernels, step(): pl.pallas_call(functools.partial(kernel, side), out_shape=[jax.ShapeDtype...  379 us

profile of v2, /device:TPU:97, one launch (start us, length us, event | category | flops | bytes accessed | tf_op | source)
XLA Modules:
  0.0 385.1 jit_solution(6972647159559780575)
XLA Ops:
  0.0 379.2 %block.1 = (f32[160,7168]{1,0:T(8,128)}, bf16[160,7168]{1,0:T(8,128)(2,1)}, bf16[160,7168]{1,0:T(8,128)(2,1)}, bf16[8,320,7168]{2,1,0:T(8,128)(2,1)}, f32[8,320,...) custom-call(bf16[160,7168]{1,0:T(8,128)(2,1)} %x.1, ...), custom_call_target="tpu_custom_call" | custom-call | flops 140928614400 | bytes 55050240 | tf_op jit(solution)/shard_map/block/pallas_call | solution.py:407
  379.2 6.0 %add_convert_fusion = bf16[160,7168]{1,0:T(8,128)(2,1)} fusion(bf16[160,7168]{1,0:T(8,128)(2,1)} %get-tuple-element.10, f32[160,7168]{1,0:T(8,128)} %get-tuple-element.8, bf16[160,7168]{1,0:T(8,128)(2,1)} %get-tuple-element.9), kind=kLoop, calls=%fused_computation | loop fusion | flops 5734400 | bytes 11468800 | tf_op jit(solution)/shard_map/convert_element_type | solution.py:438

commit v3 on v2

--- a/solution.py
+++ b/solution.py
@@ -10,6 +10,7 @@
 
 OFF = (0, 1, -1, 2)
 PLUS, MINUS = 1, 2
+LATE = 1536
 UNITS = 8
 VMEM_LIMIT = 67043328
 
@@ -42,7 +43,7 @@
             for k in range(4):
                 for m in (1, 2, 3):
                     ids(("ra", h, k, d, m))
-            for m in (1, 2, 3):
+            for m in (1, 2, 3, 4):
                 ids(("rb", h, d, m))
     return ids.ids
 
@@ -52,13 +53,13 @@
 
 def kernel(
     side, x, wg_hbm, wu_hbm, wd_hbm,
-    own_sum, low, high, xg, tf, tb, a1, bx, m3, rf, rb, a1b, m3b,
-    wg, wu, wd, xbuf, hid, stg, half_stg, fa, wsem, xsem, osem, ssem, lsem, send, recv,
+    early, most, late, xg, tf, tb, a1, bx, m3, rf, rb, a1b, m3b, mid, near,
+    wg, wu, wd, xbuf, hid, stg, half_stg, fa, wsem, xsem, osem, ssem, lsem, zsem, send, recv,
 ):
     half, depth = x.shape[0] // 2, x.shape[1]
     piece = depth // 2
+    soon = piece - LATE
     ff = wg_hbm.shape[1]
-    sides = (low, high)
     me = lax.axis_index("tp")
     mx, my = me // side, me % side
 
@@ -110,9 +111,12 @@
             if m == 1:
                 src, dst = rb.at[h, 3, :, col(d)], a1b.at[h, d]
             elif m == 2:
-                src, dst = rb.at[h, here, :, col(1 - d)], sides[d].at[rows(h), col(1 - d)]
+                src, dst = rb.at[h, here, :, col(1 - d)], mid.at[h, d]
+            elif m == 3:
+                src, dst = m3b.at[h, d, :, pl.ds(0, soon)], near.at[h, d]
             else:
-                src, dst = m3b.at[h, d], sides[d].at[rows(h), col(d)]
+                src = m3b.at[h, d, :, pl.ds(soon, LATE)]
+                dst = late.at[rows(h), pl.ds(d * LATE, LATE)]
         i = IDS[key]
         return pltpu.make_async_remote_copy(
             src_ref=src,
@@ -264,24 +268,26 @@
 
     quarter = fa.shape[2]
 
-    def room(i):
-        return rows(i // 4), pl.ds((i % 4) * quarter, quarter)
-
-    def combine(items):
+    def combine(items, wide_columns=piece):
+        step = min(quarter, wide_columns)
+
+        def room(i):
+            return rows(i // 4), pl.ds((i % 4) * quarter, step)
+
         parts = []
         for wide, narrow, to_wide, to_narrow, then in items:
-            for q in (0, 1):
-                c = pl.ds(q * quarter, quarter)
+            for q in range(wide_columns // step):
+                c = pl.ds(q * step, step)
                 cut = lambda ref: None if ref is None else ref.at[:, c]
                 parts.append((
                     cut(wide), [cut(r) for r in narrow], cut(to_wide), cut(to_narrow),
-                    then if q == 1 else None,
+                    then if q == wide_columns // step - 1 else None,
                 ))
 
         def loads(i):
             wide, narrow = parts[i][:2]
             s = i % 2
-            out = [pltpu.make_async_copy(wide, fa.at[s], lsem.at[3 * s])]
+            out = [pltpu.make_async_copy(wide, fa.at[s, :, pl.ds(0, step)], lsem.at[3 * s])]
             for n, ref in enumerate(narrow):
                 out.append(pltpu.make_async_copy(
                     ref, xbuf.at[room(3 * s + n)], lsem.at[3 * s + 1 + n]))
@@ -292,7 +298,7 @@
             s = i % 2
             out = []
             if wide is not None:
-                out.append(pltpu.make_async_copy(fa.at[s], wide, osem.at[s]))
+                out.append(pltpu.make_async_copy(fa.at[s, :, pl.ds(0, step)], wide, osem.at[s]))
             if narrow is not None:
                 out.append(pltpu.make_async_copy(xbuf.at[room(3 * s + 2)], narrow, ssem.at[s]))
             return out
@@ -314,11 +320,11 @@
                     c.start()
             for c in loads(i):
                 c.wait()
-            total = fa[s]
+            total = fa[s, :, :step]
             for n in range(len(parts[i][1])):
                 total = total + xbuf[room(3 * s + n)].astype(jnp.float32)
             if parts[i][2] is not None:
-                fa[s] = total
+                fa[s, :, :step] = total
             if parts[i][3] is not None:
                 xbuf[room(3 * s + 2)] = total.astype(jnp.bfloat16)
             for c in stores(i):
@@ -344,8 +350,7 @@
             (
                 blk(tf, h, k, 0, c),
                 [bx.at[h, k, 0, :, col(c)], bx.at[h, k, 1, :, col(c)]],
-                (own_sum.at[rows(h), col(c)] if k == 0 else rf.at[h, k, :, col(c)])
-                if c in wide else None,
+                rf.at[h, k, :, col(c)] if c in wide else None,
                 rb.at[h, k, :, col(c)] if c in narrow else None,
                 then(h, c),
             )
@@ -373,10 +378,109 @@
         for h, d in both
     ])
     for h, d in both:
-        for m in (2, 3):
-            message(("rb", h, d, m)).wait_recv()
+        message(("rb", h, d, 4)).start()
+
+    for h, d in both:
+        message(("rb", h, d, 2)).wait_recv()
+    width = n_down
+    spots = [(h, c, q) for h in (0, 1) for c in (0, 1) for q in range(soon // width)]
+
+    def spot(i):
+        h, c, q = spots[i]
+        return q, rows(2 * h + c)
+
+    def lane(i):
+        h, c, q = spots[i]
+        return rows(2 * h + c), pl.ds(q * width, width)
+
+    def fetch(i):
+        h, c, q = spots[i]
+        return (
+            pltpu.make_async_copy(
+                rf.at[h, 0, :, pl.ds(c * piece + q * width, width)], stg.at[spot(i)], zsem.at[i]),
+            pltpu.make_async_copy(
+                mid.at[h, 1 - c, :, pl.ds(q * width, width)], xbuf.at[lane(i)],
+                zsem.at[len(spots) + i]),
+        )
+
+    for i in range(len(spots)):
+        for c in fetch(i):
+            c.start()
+    for i in range(len(spots)):
+        for c in fetch(i):
+            c.wait()
+        stg[spot(i)] = stg[spot(i)] + xbuf[lane(i)].astype(jnp.float32)
+    combine([
+        (
+            rf.at[h, 0, :, pl.ds(c * piece + soon, LATE)],
+            [mid.at[h, 1 - c, :, pl.ds(soon, LATE)]],
+            most.at[rows(h), pl.ds(c * LATE, LATE)], None, None,
+        )
+        for h in (0, 1) for c in (0, 1)
+    ], LATE)
+    for h, d in both:
+        message(("rb", h, d, 3)).wait_recv()
+
+    def arrived(i):
+        h, c, q = spots[i]
+        return pltpu.make_async_copy(
+            near.at[h, c, :, pl.ds(q * width, width)], xbuf.at[lane(i)], zsem.at[i])
+
+    def settled(i):
+        h, c, q = spots[i]
+        return pltpu.make_async_copy(
+            xbuf.at[lane(i)], early.at[rows(h), pl.ds(c * soon + q * width, width)],
+            zsem.at[len(spots) + i])
+
+    for i in range(len(spots)):
+        arrived(i).start()
+    for i in range(len(spots)):
+        arrived(i).wait()
+        total = stg[spot(i)] + xbuf[lane(i)].astype(jnp.float32)
+        xbuf[lane(i)] = total.astype(jnp.bfloat16)
+        settled(i).start()
+    for i in range(len(spots)):
+        settled(i).wait()
+    for h, d in both:
+        message(("rb", h, d, 4)).wait_recv()
     for key in IDS:
         message(key).wait_send()
+
+
+def finish(early, most, late, y, rest, add, out, sem):
+    rows, columns = most.shape
+    piece, soon, cut = y.shape[1] // 2, early.shape[1] // 2, rows // 2
+    spots = [(i, c) for i in (0, 1) for c in (0, 1)]
+
+    def part(i, c, n):
+        r = pl.ds(i * cut, cut)
+        place = (r, pl.ds(c * piece, soon))
+        lane = (r, pl.ds(c * LATE, LATE))
+        to = (r, pl.ds(c * piece + soon, LATE))
+        src, dst = (
+            (most.at[lane], rest.at[lane]),
+            (late.at[lane], add.at[lane]),
+            (early.at[r, pl.ds(c * soon, soon)], out.at[place]),
+            (out.at[place], y.at[place]),
+            (out.at[to], y.at[to]),
+        )[n]
+        return pltpu.make_async_copy(src, dst, sem.at[5 * (2 * i + c) + n])
+
+    for i, c in spots:
+        for n in (0, 1, 2):
+            part(i, c, n).start()
+    for i, c in spots:
+        part(i, c, 0).wait()
+        part(i, c, 1).wait()
+        r, lane = pl.ds(i * cut, cut), pl.ds(c * LATE, LATE)
+        total = rest[r, lane] + add[r, lane].astype(jnp.float32)
+        out[r, pl.ds(c * piece + soon, LATE)] = total.astype(out.dtype)
+        part(i, c, 4).start()
+        part(i, c, 2).wait()
+        part(i, c, 3).start()
+    for i, c in spots:
+        part(i, c, 3).wait()
+        part(i, c, 4).wait()
 
 
 def solution(mesh):
@@ -390,9 +494,9 @@
         n = len(IDS)
         flops = 6 * rows * side * side * depth * ff
         shapes = [
-            ((rows, depth), f32),
-            ((rows, depth), bf),
-            ((rows, depth), bf),
+            ((rows, depth - 2 * LATE), bf),
+            ((rows, 2 * LATE), f32),
+            ((rows, 2 * LATE), bf),
             ((UNITS, 4 * half, depth), bf),
             ((UNITS, 4 * half, depth), f32),
             ((UNITS, 4 * half, depth), bf),
@@ -403,6 +507,8 @@
             ((2, 4, half, depth), bf),
             ((2, 2, half, piece), bf),
             ((2, 2, half, piece), bf),
+            ((2, 2, half, piece), bf),
+            ((2, 2, half, piece - LATE), bf),
         ]
         out = pl.pallas_call(
             functools.partial(kernel, side),
@@ -423,6 +529,7 @@
                 pltpu.SemaphoreType.DMA((2,)),
                 pltpu.SemaphoreType.DMA((2,)),
                 pltpu.SemaphoreType.DMA((6,)),
+                pltpu.SemaphoreType.DMA((16,)),
                 pltpu.SemaphoreType.DMA((n,)),
                 pltpu.SemaphoreType.DMA((n,)),
             ],
@@ -434,8 +541,20 @@
             ),
             name="block",
         )(x, w_gate, w_up, w_down)
-        own_sum, low, high = out[:3]
-        return (own_sum + low.astype(f32) + high.astype(f32)).astype(bf)
+        return pl.pallas_call(
+            finish,
+            out_shape=jax.ShapeDtypeStruct((rows, depth), bf),
+            in_specs=[pl.BlockSpec(memory_space=pl.ANY)] * 3,
+            out_specs=pl.BlockSpec(memory_space=pl.ANY),
+            scratch_shapes=[
+                pltpu.VMEM((rows, 2 * LATE), f32),
+                pltpu.VMEM((rows, 2 * LATE), bf),
+                pltpu.VMEM((rows, depth), bf),
+                pltpu.SemaphoreType.DMA((20,)),
+            ],
+            compiler_params=pltpu.CompilerParams(vmem_limit_bytes=VMEM_LIMIT),
+            name="finish",
+        )(*out[:3])
 
     return jax.shard_map(
         step,

time: 386 us -> 384 us (level)
  other arithmetic: 5.96 us -> 0 us
  Pallas kernels: 379 us -> 383 us
    convert_element_type x1 -> x0, other arithmetic: 5.96 us -> none  [step(): return (own_sum + low.astype(f32) + high.astype(f32)).astype(bf)]
where the time goes in v3:
time: 384 us; the launch traced here: 383 us
  Pallas kernels  383 us (100%)
    pallas_call x1, Pallas kernels, step(): pl.pallas_call(functools.partial(kernel, side), out_shape=[jax.ShapeDtype...  379 us

profile of v3, /device:TPU:97, one launch (start us, length us, event | category | flops | bytes accessed | tf_op | source)
XLA Modules:
  0.0 382.8 jit_solution(16538008927286895151)
XLA Ops:
  0.0 379.4 %block.1 = (bf16[160,4096]{1,0:T(8,128)(2,1)}, f32[160,3072]{1,0:T(8,128)}, bf16[160,3072]{1,0:T(8,128)(2,1)}, bf16[8,320,7168]{2,1,0:T(8,128)(2,1)}, f32[8,320,...) custom-call(bf16[160,7168]{1,0:T(8,128)(2,1)} %x.1, ...), custom_call_target="tpu_custom_call" | custom-call | flops 140928614400 | bytes 55050240 | tf_op jit(solution)/shard_map/block/pallas_call | solution.py:513
  379.4 3.4 finish.1

commit v4 on v3

--- a/solution.py
+++ b/solution.py
@@ -54,7 +54,7 @@
 def kernel(
     side, x, wg_hbm, wu_hbm, wd_hbm,
     early, most, late, xg, tf, tb, a1, bx, m3, rf, rb, a1b, m3b, mid, near,
-    wg, wu, wd, xbuf, hid, stg, half_stg, fa, wsem, xsem, osem, ssem, lsem, zsem, send, recv,
+    wg, wu, wd, xbuf, hid, stg, half_stg, fa, wsem, xsem, osem, ssem, lsem, zsem, below, send, recv,
 ):
     half, depth = x.shape[0] // 2, x.shape[1]
     piece = depth // 2
@@ -130,16 +130,25 @@
     both = [(h, d) for h in (0, 1) for d in (0, 1)]
 
     barrier = pltpu.get_barrier_semaphore()
-    for h, d in both:
+    for h in (0, 1):
         pl.semaphore_signal(
-            barrier, inc=1, device_id={"tp": peer(h, False, d)},
+            barrier, inc=1, device_id={"tp": peer(h, False, 1)},
             device_id_type=pl.DeviceIdType.MESH,
         )
-    pl.semaphore_wait(barrier, 4)
+    pl.semaphore_wait(barrier, 2)
+    for h in (0, 1):
+        pl.semaphore_signal(
+            below.at[h], inc=1, device_id={"tp": peer(h, False, 0)},
+            device_id_type=pl.DeviceIdType.MESH,
+        )
 
     for n in (0, 1):
-        for h, d in both:
-            message(("a", h, d, (d + n) % 2)).start()
+        for h in (0, 1):
+            message(("a", h, 0, n)).start()
+    for h in (0, 1):
+        pl.semaphore_wait(below.at[h], 1)
+        for n in (0, 1):
+            message(("a", h, 1, 1 - n)).start()
     weights = [
         pltpu.make_async_copy(src, dst, wsem.at[i])
         for i, (src, dst) in enumerate(((wg_hbm, wg), (wu_hbm, wu), (wd_hbm, wd)))
@@ -441,9 +450,13 @@
         settled(i).start()
     for i in range(len(spots)):
         settled(i).wait()
-    for h, d in both:
-        message(("rb", h, d, 4)).wait_recv()
+    last = [("rb", h, d, 4) for h, d in both]
     for key in IDS:
+        if key not in last:
+            message(key).wait_send()
+    for key in last:
+        message(key).wait_recv()
+    for key in last:
         message(key).wait_send()
 
 
@@ -530,6 +543,7 @@
                 pltpu.SemaphoreType.DMA((2,)),
                 pltpu.SemaphoreType.DMA((6,)),
                 pltpu.SemaphoreType.DMA((16,)),
+                pltpu.SemaphoreType.REGULAR((2,)),
                 pltpu.SemaphoreType.DMA((n,)),
                 pltpu.SemaphoreType.DMA((n,)),
             ],

time: 384 us -> 383 us (level)
  no operation moved by 1% of the time
where the time goes in v4:
time: 383 us; the launch traced here: 382 us
  Pallas kernels  382 us (100%)
    pallas_call x1, Pallas kernels, step(): pl.pallas_call(functools.partial(kernel, side), out_shape=[jax.ShapeDtype...  378 us

profile of v4, /device:TPU:97, one launch (start us, length us, event | category | flops | bytes accessed | tf_op | source)
XLA Modules:
  0.0 381.6 jit_solution(9650293160989461385)
XLA Ops:
  0.0 378.3 %block.1 = (bf16[160,4096]{1,0:T(8,128)(2,1)}, f32[160,3072]{1,0:T(8,128)}, bf16[160,3072]{1,0:T(8,128)(2,1)}, bf16[8,320,7168]{2,1,0:T(8,128)(2,1)}, f32[8,320,...) custom-call(bf16[160,7168]{1,0:T(8,128)(2,1)} %x.1, ...), custom_call_target="tpu_custom_call" | custom-call | flops 140928614400 | bytes 55050240 | tf_op jit(solution)/shard_map/block/pallas_call | solution.py:526
  378.3 3.4 finish.1

commit v5 on v4

--- a/solution.py
+++ b/solution.py
@@ -11,6 +11,7 @@
 OFF = (0, 1, -1, 2)
 PLUS, MINUS = 1, 2
 LATE = 1536
+CUTS = 5
 UNITS = 8
 VMEM_LIMIT = 67043328
 
@@ -462,8 +463,8 @@
 
 def finish(early, most, late, y, rest, add, out, sem):
     rows, columns = most.shape
-    piece, soon, cut = y.shape[1] // 2, early.shape[1] // 2, rows // 2
-    spots = [(i, c) for i in (0, 1) for c in (0, 1)]
+    piece, soon, cut = y.shape[1] // 2, early.shape[1] // 2, rows // CUTS
+    spots = [(i, c) for i in range(CUTS) for c in (0, 1)]
 
     def part(i, c, n):
         r = pl.ds(i * cut, cut)
@@ -480,8 +481,13 @@
         return pltpu.make_async_copy(src, dst, sem.at[5 * (2 * i + c) + n])
 
     for i, c in spots:
-        for n in (0, 1, 2):
+        part(i, c, 2).start()
+    for i, c in spots:
+        for n in (0, 1):
             part(i, c, n).start()
+    for i, c in spots:
+        part(i, c, 2).wait()
+        part(i, c, 3).start()
     for i, c in spots:
         part(i, c, 0).wait()
         part(i, c, 1).wait()
@@ -489,8 +495,6 @@
         total = rest[r, lane] + add[r, lane].astype(jnp.float32)
         out[r, pl.ds(c * piece + soon, LATE)] = total.astype(out.dtype)
         part(i, c, 4).start()
-        part(i, c, 2).wait()
-        part(i, c, 3).start()
     for i, c in spots:
         part(i, c, 3).wait()
         part(i, c, 4).wait()
@@ -564,7 +568,7 @@
                 pltpu.VMEM((rows, 2 * LATE), f32),
                 pltpu.VMEM((rows, 2 * LATE), bf),
                 pltpu.VMEM((rows, depth), bf),
-                pltpu.SemaphoreType.DMA((20,)),
+                pltpu.SemaphoreType.DMA((10 * CUTS,)),
             ],
             compiler_params=pltpu.CompilerParams(vmem_limit_bytes=VMEM_LIMIT),
             name="finish",

time: 383 us -> 384 us (level)
  no operation moved by 1% of the time
where the time goes in v5:
time: 384 us; the launch traced here: 382 us
  Pallas kernels  382 us (99%)
    pallas_call x1, Pallas kernels, step(): pl.pallas_call(functools.partial(kernel, side), out_shape=[jax.ShapeDtype...  378 us

profile of v5, /device:TPU:97, one launch (start us, length us, event | category | flops | bytes accessed | tf_op | source)
XLA Modules:
  0.0 382.3 jit_solution(13739384453457872699)
XLA Ops:
  0.0 378.3 %block.1 = (bf16[160,4096]{1,0:T(8,128)(2,1)}, f32[160,3072]{1,0:T(8,128)}, bf16[160,3072]{1,0:T(8,128)(2,1)}, bf16[8,320,7168]{2,1,0:T(8,128)(2,1)}, f32[8,320,...) custom-call(bf16[160,7168]{1,0:T(8,128)(2,1)} %x.1, ...), custom_call_target="tpu_custom_call" | custom-call | flops 140928614400 | bytes 55050240 | tf_op jit(solution)/shard_map/block/pallas_call | solution.py:530
  378.3 4.0 %finish.1 = bf16[160,7168]{1,0:T(8,128)(2,1)} custom-call(bf16[160,4096]{1,0:T(8,128)(2,1)} %get-tuple-element.8.early, f32[160,3072]{1,0:T(8,128)} %get-tuple-element.9.most, bf16[160,3072]{1,0:T(8,128)(2,1)} %get-tuple-element.10.late), custom_call_target="tpu_custom_call" | custom-call | tf_op jit(solution)/shard_map/finish/pallas_call | solution.py:562
